TPU v7x, 32 devices: a whole 2x2x4 slice. The times are simulated.
32 devices in a mesh: grp: 2 (over y), seq: 4 (over z), head: 2 (over x), rep: 2 (over core).
Axes of the slice: x: 2, y: 2, z: 4, core: 2. Of those that a mesh axis runs over, the one named last changes fastest.
Arguments:
- x_proj: bfloat16 [4, 4, 4, 32, 8192], P(('grp', 'rep'), None, 'seq', None, 'head'), parts along dimension 0, may hold values from -6 to 6
- gate_proj: bfloat16 [4, 4, 4, 32, 8192], P(('grp', 'rep'), None, 'seq', None, 'head'), parts along dimension 0, may hold values from -6 to 6
- bc_proj: bfloat16 [4, 4, 4, 32, 256], P(('grp', 'rep'), None, 'seq'), parts along dimension 0, may hold values from -6 to 6
- dt_proj: bfloat16 [4, 4, 4, 32, 128], P(('grp', 'rep'), None, 'seq', None, 'head'), parts along dimension 0, may hold values from -5.5 to 7.5
- a_rate: float32 [128], P('head'), may hold values from 0.0001953125 to 0.05
- dt_bias: float32 [128], P('head'), may hold values from -1 to 1
- d_skip: float32 [128], P('head'), may hold values from 0.5 to 1.5
- conv_x_weight: float32 [4, 8192], P(None, 'head'), may hold values from -3 to 3
- conv_bc_weight: float32 [4, 256], replicated, may hold values from -3 to 3
- norm_gain: float32 [8192], P('head'), may hold values from 0.1 to 1.9
- out_weight: bfloat16 [8192, 2048], P(('seq', 'rep'), 'head'), may hold values from -0.0625 to 0.0625
- request_first_position: int32 [4], P(('grp', 'rep')), parts along dimension 0, may hold values from 0 to 255
- owner: int32 [4, 4], P(('grp', 'rep')), parts along dimension 0, may hold values from 0 to 3, each once within a row
Outputs:
- mixed: bfloat16 [4, 512, 2048], P(('grp', 'rep'), 'seq', 'head'), parts along dimension 0
- ssm_state: float32 [4, 4, 128, 2048], P(('grp', 'rep'), 'seq', 'head'), parts along dimension 0
- conv_x_state: bfloat16 [4, 4, 3, 2048], P(('grp', 'rep'), 'seq', None, 'head'), parts along dimension 0
- conv_bc_state: bfloat16 [4, 4, 3, 64], P(('grp', 'rep'), 'seq'), parts along dimension 0
There are 2 independent parts, one for each index of `grp`. A program takes and returns all parts, laid end to end along the dimension named above; an argument that names none is the same for every part. Nothing has to cross between parts.
Inputs may be any that keep to these rules, and one draw needn't show every extreme that they name: Each row of owner names every index of seq once.
All inputs are finite; a program needn't handle non-finite values.
Results may differ from a plain program's by a relative error of at most 0.007.
Values may be sent and summed in bfloat16 or wider, within the bound.
A program may use at most 128 MiB of HBM per device.

v0:
```python
import jax
import jax.numpy as jnp
from jax import lax
from jax.sharding import PartitionSpec as P

HEAD_DIM = 64
NSTATE = 128
KCONV = 4
SPAN = 128
INNER = 8192
highest = lax.Precision.HIGHEST
stability_constant = 1e-05


def passed_along(value, axis, by):
    devices = lax.axis_size(axis)
    pairs = [(i, i + by) for i in range(devices) if 0 <= i + by < devices]
    return lax.ppermute(value, axis, pairs)


def prefix(value, axis, combine, identity, reverse):
    devices, place = (lax.axis_size(axis), lax.axis_index(axis))
    everything = jax.tree.map(lambda part: lax.all_gather(part, axis), value)
    start = jax.tree.map(
        lambda part, zero: jnp.broadcast_to(jnp.asarray(zero, part.dtype), part.shape),
        value,
        identity,
    )

    def lap(k, before):
        at = devices - 1 - k if reverse else k
        reached = at > place if reverse else at < place
        new = combine(before, jax.tree.map(lambda part: part[at], everything))
        return jax.tree.map(lambda a, b: jnp.where(reached, a, b), new, before)

    return lax.fori_loop(0, devices, lap, start)


def broadcast(block, axis, source):
    block = jnp.where(lax.axis_index(axis) == source, block, jnp.zeros_like(block))
    return lax.psum(block, axis)


def span_terms(x_conv, b_rows, c_rows, step_size, log_decay):
    cum_decay = jnp.cumsum(log_decay, axis=1)
    scores = jnp.einsum("kqn,ktn->kqt", c_rows, b_rows, preferred_element_type=jnp.float32)
    cum_heads = jnp.swapaxes(cum_decay, 1, 2)
    step_heads = jnp.swapaxes(step_size, 1, 2)
    block_len = cum_decay.shape[1]
    causal = jnp.arange(block_len)[:, None] >= jnp.arange(block_len)[None, :]
    decay_gap = cum_heads[:, :, :, None] - cum_heads[:, :, None, :]
    seg_decay = jnp.exp(jnp.where(causal, decay_gap, -jnp.inf))
    weights = (scores[:, None] * seg_decay * step_heads[:, :, None, :]).astype(jnp.bfloat16)
    y_intra = jnp.einsum("khqt,kthp->kqhp", weights, x_conv, preferred_element_type=jnp.float32)
    remaining_length = jnp.exp(cum_decay[:, -1:, :] - cum_decay)
    scaled = ((remaining_length * step_size)[..., None] * x_conv.astype(jnp.float32)).astype(
        jnp.bfloat16
    )
    states = jnp.einsum("kthp,ktn->khpn", scaled, b_rows, preferred_element_type=jnp.float32)
    return (cum_decay, y_intra, states, jnp.exp(cum_decay[:, -1, :]))


def conv_silu(preceding_tokens, current, weight):
    extended = jnp.concatenate([preceding_tokens, current], axis=0)
    length = current.shape[0]
    accum = jnp.zeros(current.shape, jnp.float32)
    for offset in range(weight.shape[0]):
        accum = accum + weight[offset] * extended[offset : offset + length].astype(jnp.float32)
    return jax.nn.silu(accum)


def link(preceding_tokens, later):
    return (
        preceding_tokens[0] * later[0],
        later[0][:, None, None] * preceding_tokens[1] + later[1],
    )


def multiply(preceding_tokens, later):
    return preceding_tokens * later


def add_rows(source, piece):
    return jnp.dot(source, piece, preferred_element_type=jnp.float32)


def take_slab(values, slab_index, seq_count):
    grouped = values.reshape(values.shape[0], seq_count, -1)
    return lax.dynamic_index_in_dim(grouped, slab_index, axis=1, keepdims=False)


def local(
    x_proj,
    gate_proj,
    bc_proj,
    dt_proj,
    a_rate,
    dt_bias,
    d_skip,
    conv_x_weight,
    conv_bc_weight,
    norm_gain,
    out_weight,
    request_first_position,
    owner,
):
    x_all, z_all, bc_all, dt_all = (
        lax.all_to_all(x_proj, "seq", split_axis=1, concat_axis=2, tiled=True),
        lax.all_to_all(gate_proj, "seq", split_axis=1, concat_axis=2, tiled=True),
        lax.all_to_all(bc_proj, "seq", split_axis=1, concat_axis=2, tiled=True),
        lax.all_to_all(dt_proj, "seq", split_axis=1, concat_axis=2, tiled=True),
    )
    tokens_here = x_all.shape[2] * x_all.shape[3]
    x_local = x_all.reshape(tokens_here, x_all.shape[4])
    z_local = z_all.reshape(tokens_here, z_all.shape[4])
    bc_local = bc_all.reshape(tokens_here, bc_all.shape[4])
    dt_local = dt_all.reshape(tokens_here, dt_all.shape[4])
    heads = dt_local.shape[1]
    seq_index = lax.axis_index("seq")
    seq_count = lax.axis_size("seq")
    positions = seq_index * tokens_here + jnp.arange(tokens_here, dtype=jnp.int32)
    is_live = positions >= request_first_position[0]
    x_live = jnp.where(is_live[:, None], x_local, jnp.zeros_like(x_local))
    bc_live = jnp.where(is_live[:, None], bc_local, jnp.zeros_like(bc_local))
    rim_rows = KCONV - 1
    tail_x = x_live[tokens_here - rim_rows :]
    tail_bc = bc_live[tokens_here - rim_rows :]
    before_x, before_bc = passed_along((tail_x, tail_bc), "seq", 1)
    x_conv = conv_silu(before_x, x_live, conv_x_weight).astype(jnp.bfloat16)
    bc_conv = conv_silu(before_bc, bc_live, conv_bc_weight).astype(jnp.bfloat16)
    step_size = (
        jax.nn.softplus(dt_local.astype(jnp.float32) + dt_bias)
        * is_live.astype(jnp.float32)[:, None]
    )
    log_decay = -a_rate * step_size
    blocks = tokens_here // SPAN
    x_blocks = x_conv.reshape(blocks, SPAN, heads, HEAD_DIM)
    b_blocks = bc_conv[:, :NSTATE].reshape(blocks, SPAN, NSTATE)
    c_blocks = bc_conv[:, NSTATE:].reshape(blocks, SPAN, NSTATE)
    cum_decay, y_intra, states, decays = span_terms(
        x_blocks,
        b_blocks,
        c_blocks,
        step_size.reshape(blocks, SPAN, heads),
        log_decay.reshape(blocks, SPAN, heads),
    )

    def advance(carry, inputs):
        factor, contrib = inputs
        return (factor[:, None, None] * carry + contrib, carry)

    zero_state = jnp.zeros((heads, HEAD_DIM, NSTATE), jnp.float32)
    local_final, local_enter = lax.scan(advance, zero_state, (decays, states))
    dev_decay = jnp.prod(decays, axis=0)
    ones_heads = jnp.ones((heads,), jnp.float32)
    enter_decay, enter_state = prefix(
        (dev_decay, local_final), "seq", link, (ones_heads, zero_state), False
    )
    c_wide = c_blocks.astype(jnp.float32)
    before_block = jnp.concatenate([ones_heads[None], jnp.cumprod(decays, axis=0)[:-1]], axis=0)
    entering = local_enter + before_block[:, :, None, None] * enter_state[None]
    y_state = jnp.exp(cum_decay)[..., None] * jnp.einsum(
        "kqn,khpn->kqhp", c_wide, entering, precision=highest
    )
    y_total = y_intra + y_state + d_skip[:, None] * x_blocks.astype(jnp.float32)
    y_flat = y_total.reshape(tokens_here, heads * HEAD_DIM)
    gated = y_flat * jax.nn.silu(z_local.astype(jnp.float32))
    square_sums = lax.psum(jnp.sum(gated * gated, axis=1), "head")
    normed = (
        gated * lax.rsqrt(square_sums[:, None] / INNER + stability_constant) * norm_gain
    ).astype(jnp.bfloat16)
    last_index = seq_count - 1
    after_decay = prefix(dev_decay, "seq", multiply, ones_heads, True)
    final_state = lax.psum(after_decay[:, None, None] * local_final, "seq")
    keep_x, keep_bc = (broadcast(tail_x, "seq", last_index), broadcast(tail_bc, "seq", last_index))
    slab_index = jnp.sum(
        jnp.where(owner[0] == seq_index, jnp.arange(seq_count, dtype=jnp.int32), 0)
    )
    ssm_state = take_slab(final_state.reshape(heads, -1), slab_index, seq_count)[None, None]
    conv_x_state = take_slab(keep_x, slab_index, seq_count)[None, None]
    conv_bc_state = take_slab(keep_bc, slab_index, seq_count)[None, None]
    features = lax.all_gather(normed, "head", axis=1, tiled=True)
    out_cols = out_weight.shape[1]
    mixed_sum = add_rows(features, lax.all_gather(out_weight, ("seq", "rep"), axis=0, tiled=True))
    mixed = mixed_sum.astype(jnp.bfloat16).reshape(1, tokens_here, out_cols)
    return (mixed, ssm_state, conv_x_state, conv_bc_state)


def solution(mesh):
    return jax.shard_map(
        local,
        mesh=mesh,
        in_specs=(
            P(("grp", "rep"), None, "seq", None, "head"),
            P(("grp", "rep"), None, "seq", None, "head"),
            P(("grp", "rep"), None, "seq", None, None),
            P(("grp", "rep"), None, "seq", None, "head"),
            P("head"),
            P("head"),
            P("head"),
            P(None, "head"),
            P(),
            P("head"),
            P(("seq", "rep"), "head"),
            P(("grp", "rep")),
            P(("grp", "rep"), None),
        ),
        out_specs=(
            P(("grp", "rep"), "seq", "head"),
            P(("grp", "rep"), "seq", "head", None),
            P(("grp", "rep"), "seq", None, "head"),
            P(("grp", "rep"), "seq", None, None),
        ),
        check_vma=False,
    )
```

profile of v0, /device:TPU:0, one launch (start us, length us, event | category | flops | bytes accessed | tf_op | source)
XLA Modules:
  0.0 532.8 jit_solution(8478039113186121479)
XLA Ops:
  7.2 0.7 copy-done
  7.9 0.7 reshape.454
  8.6 6.3 %all-to-all-start.2 = ((bf16[4,2,1024]{2,1,0:T(2,128)(2,1)}), bf16[4,2,1024]{2,1,0:T(2,128)(2,1)S(1)}, u32[]{:S(2)}, u32[]{:S(2)}) async-start(bf16[4,2,1024]{2,1,0:T(2,128)(2,1)} %reshape.454), calls=%async_computation.2 | async-start | bytes 32768 | tf_op jit(solution)/shard_map/all_to_all | solution.py:111
  15.6 1.7 fusion.36
  17.3 1.4 fusion.37
  20.6 4.5 all-to-all-start.1
  25.2 0.7 broadcast_multiply_fusion.1
  26.1 0.7 bitcast_exponential_fusion
  27.1 1.9 copy.80
  29.0 11.5 %all-gather = f32[4,1,64]{2,1,0:T(1,128)S(1)} all-gather(f32[1,1,64]{2,1,0:T(1,128)S(1)} %get-tuple-element.290), channel_id=2, replica_groups=mesh['grp'=2,'seq'=4,'head'=2,'rep'=2] {'seq'}, dimensions={0}, use_global_device_ids=true | all-gather | bytes 1280 | tf_op jit(solution)/shard_map/all_gather | solution.py:23
  40.5 3.7 all-to-all-start
  45.0 0.9 bitcast_select_fusion.1
  46.6 3.8 collective-permute-start.1
  50.4 16.6 %all-to-all-done = bf16[1,4,1,32,4096]{4,3,2,0,1:T(8,128)(2,1)S(1)} async-done(((bf16[1,4,1,32,4096]{4,3,2,0,1:T(8,128)(2,1)}), bf16[1,4,1,32,4096]{4,3,2,0,1:T(8,128)(2,1)S(1)}, u32[]{:S(2)}, u32[]{:S(2)}) %all-to-all-start) | async-done | bytes 1048608 | tf_op jit(solution)/shard_map/all_to_all | solution.py:108
  67.3 1.3 collective-permute-start
  69.2 0.9 multiply_convert_fusion.4
  70.2 3.1 multiply_convert_fusion.2
  73.3 1.6 copy.81
  74.9 2.4 broadcast_multiply_fusion
  77.3 5.7 %all-to-all-start.3 = ((bf16[1,4,1,32,4096]{4,3,2,0,1:T(8,128)(2,1)}), bf16[1,4,1,32,4096]{4,3,2,0,1:T(8,128)(2,1)}, u32[]{:S(2)}, u32[]{:S(2)}) async-start(bf16[1,4,1,32,4096]{4,3,2,0,1:T(8,128)(2,1)} %bitcast.35), calls=%async_computation.3 | async-start | bytes 2097152 | tf_op jit(solution)/shard_map/all_to_all | solution.py:109
  83.5 48.3 %all-to-all-done.3 = bf16[1,4,1,32,4096]{4,3,2,0,1:T(8,128)(2,1)} async-done(((bf16[1,4,1,32,4096]{4,3,2,0,1:T(8,128)(2,1)}), bf16[1,4,1,32,4096]{4,3,2,0,1:T(8,128)(2,1)}, u32[]{:S(2)}, u32[]{:S(2)}) %all-to-all-start.3) | async-done | bytes 1048608 | tf_op jit(solution)/shard_map/all_to_all | solution.py:109
  131.8 2.7 bitcast_convert_fusion
  134.6 4.6 reshape.449
  139.2 4.8 copy.87
  144.0 1.3 copy.72
  145.3 1.7 copy.82
  147.0 3.0 reshape_reshape.3
  150.0 1.1 copy-done.4
  151.2 3.3 fusion.1
  154.4 87.4 %all-gather.10.cloned.1.call-done = f32[256,64,128]{2,1,0:T(8,128)} async-done(((f32[64,64,128]{2,1,0:T(8,128)}), f32[256,64,128]{2,1,0:T(8,128)}) %all-gather.10.cloned.1.call-update) | async-done | bytes 8388624 | tf_op jit(solution)/shard_map/all_gather | solution.py:23
  241.9 11.4 %while.35 = (s32[]{:T(128)}, f32[64,64,128]{2,1,0:T(8,128)S(1)}, s32[]{:T(128)}, f32[4,64]{1,0:T(4,128)}, f32[4,64,64,128]{3,2,1,0:T(8,128)}, /*index=5*/s32[]{:T(128)}, s32[]{:T(128)}) while((s32[]{:T(128)}, f32[64,64,128]{2,1,0:T(8,128)S(1)}, s32[]{:T(128)}, f32[4,64]{1,0:T(4,128)}, f32[4,64,64,128]{3,2,1,0:T(8,128)}, ...), condition=%wide.region_2.3_spmd.clone, body=%wide.region_1.2_spmd.clone.sunk | while | flops 2097156 | bytes 6292329 | solution.py:36
  241.9 0.7 dynamic-slice_bitcast_fusion.4
  242.6 2.1 fusion.44
  245.3 2.1 fusion.44
  247.4 0.7 dynamic-slice_bitcast_fusion.4
  248.1 2.3 fusion.44
  251.1 2.1 fusion.44
  253.2 5.9 %multiply_reduce_fusion = (f32[128]{0:T(128)S(1)}, f32[1,128,64,64]{1,3,2,0:T(8,128)}) fusion(f32[1,128,64,64]{1,3,2,0:T(8,128)} %copy.87, f32[1,128,64,64]{1,3,2,0:T(8,128)} %bitcast.133, f32[64]{0:T(128)S(1)} %copy-done.18, f32[64,64,128]{2,1,0:T(8,128)S(1)} %get-tuple-element.223, bf16[128,256]{1,0:T(8,128)(2,1)S(1)} %multiply_convert_fusion.4, ...), kind=kOutput, calls=%fused_computation.17 | convolution fusion | flops 811073408 | bytes 10552320 | tf_op jit(solution)/shard_map/kqn,khpn->kqhp/dot_general | solution.py:162
  259.1 3.1 copy.85
  262.2 4.9 psum.28
  267.1 3.3 fusion.14
  273.7 18.3 %all-reduce = (bf16[3,4,1024]{2,0,1:T(4,128)(2,1)S(1)}, bf16[3,4,64]{2,0,1:T(4,128)(2,1)S(1)}) all-reduce(bf16[3,4,1024]{2,0,1:T(4,128)(2,1)S(1)} %bitcast.140, bf16[3,4,64]{2,0,1:T(4,128)(2,1)S(1)} %copy.89), channel_id=1, replica_groups=mesh['grp'=2,'seq'=4,'head'=2,'rep'=2] {'seq'}, use_global_device_ids=true, to_apply=%region_9.10 | all-reduce | flops 13056 | bytes 52224 | tf_op jit(solution)/shard_map/psum | solution.py:41
  293.2 37.3 %all-reduce.3.cloned.1.call-done = f32[64,4,2048]{2,1,0:T(4,128)} async-done(((f32[64,4,2048]{2,1,0:T(4,128)}), f32[64,4,2048]{2,1,0:T(4,128)}) %all-reduce.3.cloned.1.call-update) | async-done | bytes 2097168 | tf_op jit(solution)/shard_map/psum | solution.py:174
  330.5 2.1 constant_dynamic-slice_fusion
  332.7 1.0 copy.92
  333.6 30.6 %all-gather.6.cloned.1.call-done = bf16[128,8192]{1,0:T(8,128)(2,1)} async-done(((bf16[128,4096]{1,0:T(8,128)(2,1)}), bf16[128,8192]{1,0:T(8,128)(2,1)}) %all-gather.6.cloned.1.call-update) | async-done | bytes 2097168 | tf_op jit(solution)/shard_map/all_gather | solution.py:182
  364.2 152.6 %all-gather.8.cloned.1.call-done = bf16[8192,1024]{1,0:T(8,128)(2,1)} async-done(((bf16[1024,1024]{1,0:T(8,128)(2,1)}), bf16[8192,1024]{1,0:T(8,128)(2,1)}) %all-gather.8.cloned.1.call-update) | async-done | bytes 16777232 | tf_op jit(solution)/shard_map/all_gather | solution.py:184
  516.8 9.5 %fusion.16 = bf16[1,128,1024]{2,1,0:T(8,128)(2,1)} fusion(bf16[128,8192]{1,0:T(8,128)(2,1)} %all-gather.6.cloned.1.call-done, bf16[8192,1024]{1,0:T(8,128)(2,1)} %all-gather.8.cloned.1.call-done), kind=kOutput, calls=%fused_computation.31 | convolution fusion | flops 2147614720 | bytes 19136512 | tf_op jit(solution)/shard_map/dot_general | solution.py:84
  (83 shorter events, 9.2 us)
Async XLA Ops:
  7.2 0.8 copy-start
  8.6 12.0 %all-to-all-start.2 = ((bf16[4,2,1024]{2,1,0:T(2,128)(2,1)}), bf16[4,2,1024]{2,1,0:T(2,128)(2,1)S(1)}, u32[]{:S(2)}, u32[]{:S(2)}) async-start(bf16[4,2,1024]{2,1,0:T(2,128)(2,1)} %reshape.454), calls=%async_computation.2 | async-start | bytes 32768 | tf_op jit(solution)/shard_map/all_to_all | solution.py:111
  19.3 7.5 %copy-start.11 = (f32[128]{0:T(128)}, f32[128]{0:T(128)S(1)}, u32[]{:S(2)}) copy-start(f32[128]{0:T(128)S(1)} %get-tuple-element.282) | copy-start | bytes 1540
  20.6 19.9 %all-to-all-start.1 = ((bf16[1,4,1,32,256]{4,3,2,0,1:T(8,128)(2,1)}), bf16[1,4,1,32,256]{4,3,2,0,1:T(8,128)(2,1)S(1)}, u32[]{:S(2)}, u32[]{:S(2)}) async-start(bf16[1,4,1,32,256]{4,3,2,0,1:T(8,128)(2,1)} %bitcast.145), calls=%async_computation.1 | async-start | bytes 131072 | tf_op jit(solution)/shard_map/all_to_all | solution.py:110
  29.0 15.8 %copy-start.6 = (f32[64]{0:T(128)S(1)}, f32[64]{0:T(128)}, u32[]{:S(2)}) copy-start(f32[64]{0:T(128)} %custom-call.1) | copy-start | bytes 772
  29.0 16.0 %copy-start.15 = (pred[128]{0:T(512)(128)(4,1)S(1)}, pred[128]{0:T(512)(128)(4,1)}, u32[]{:S(2)}) copy-start(pred[128]{0:T(512)(128)(4,1)} %get-tuple-element.283) | copy-start | bytes 388
  40.5 4.5 copy-start.5
  40.5 29.6 %copy-start.3 = (f32[128,4096]{1,0:T(8,128)S(1)}, f32[128,4096]{1,0:T(8,128)}, u32[]{:S(2)}) copy-start(f32[128,4096]{1,0:T(8,128)} %copy.80) | copy-start | bytes 6291460
  40.5 26.5 %all-to-all-start = ((bf16[1,4,1,32,4096]{4,3,2,0,1:T(8,128)(2,1)}), bf16[1,4,1,32,4096]{4,3,2,0,1:T(8,128)(2,1)S(1)}, u32[]{:S(2)}, u32[]{:S(2)}) async-start(bf16[1,4,1,32,4096]{4,3,2,0,1:T(8,128)(2,1)} %bitcast.135), calls=%async_computation | async-start | bytes 2097152 | tf_op jit(solution)/shard_map/all_to_all | solution.py:108
  44.2 197.7 %all-gather.10.cloned.1.call-start = ((), (), s32[]{:S(2)}) async-start(), calls=%async_computation.7 | async-start | bytes 10485760 | tf_op jit(solution)/shard_map/all_gather | solution.py:23
  45.0 22.0 %copy-start.7 = (f32[64]{0:T(128)}, f32[64]{0:T(128)S(1)}, u32[]{:S(2)}) copy-start(f32[64]{0:T(128)S(1)} %get-tuple-element.224) | copy-start | bytes 772
  45.0 22.0 %copy-start.10 = (f32[4,64]{1,0:T(4,128)}, f32[4,64]{1,0:T(4,128)S(1)}, u32[]{:S(2)}) copy-start(f32[4,64]{1,0:T(4,128)S(1)} %get-tuple-element.430) | copy-start | bytes 3076
  46.6 22.0 %collective-permute-start.1 = (bf16[3,256]{1,0:T(4,128)(2,1)S(1)}, bf16[3,256]{1,0:T(4,128)(2,1)S(1)}, u32[]{:S(2)}, u32[]{:S(2)}) collective-permute-start(bf16[3,256]{1,0:T(4,128)(2,1)S(1)} %get-tuple-element.287), channel_id=1, source_target_pairs={{0,4},{4,8},{8,12},{1,5},{5,9},{9,13},{2,6},{6,10},{10,14},{3,7},{... | collective-permute-start | bytes 4616 | tf_op jit(solution)/shard_map/ppermute | solution.py:18
  67.3 2.9 collective-permute-start
  68.6 0.6 copy-start.16
  73.3 1.6 copy-start.8
  73.3 1.6 copy-start.17
  77.3 5.7 %copy-start.12 = (f32[128]{0:T(128)S(1)}, f32[128]{0:T(128)}, u32[]{:S(2)}) copy-start(f32[128]{0:T(128)} %copy-done.11) | copy-start | bytes 1540
  77.3 5.8 %copy-start.14 = (f32[64]{0:T(128)S(1)}, f32[64]{0:T(128)}, u32[]{:S(2)}) copy-start(f32[64]{0:T(128)} %param.22) | copy-start | bytes 772
  77.3 54.5 %all-to-all-start.3 = ((bf16[1,4,1,32,4096]{4,3,2,0,1:T(8,128)(2,1)}), bf16[1,4,1,32,4096]{4,3,2,0,1:T(8,128)(2,1)}, u32[]{:S(2)}, u32[]{:S(2)}) async-start(bf16[1,4,1,32,4096]{4,3,2,0,1:T(8,128)(2,1)} %bitcast.35), calls=%async_computation.3 | async-start | bytes 2097152 | tf_op jit(solution)/shard_map/all_to_all | solution.py:109
  83.0 247.5 %all-reduce.3.cloned.1.call-start = ((), (), s32[]{:S(2)}) async-start(), calls=%async_computation.6 | async-start | bytes 4194304 | tf_op jit(solution)/shard_map/psum | solution.py:174
  149.9 1.2 copy-start.4
  150.0 214.3 %all-gather.6.cloned.1.call-start = ((), (), s32[]{:S(2)}) async-start(), calls=%async_computation.4 | async-start | bytes 3145728 | tf_op jit(solution)/shard_map/all_gather | solution.py:182
  241.9 11.4 %copy-start.18 = (f32[64]{0:T(128)S(1)}, f32[64]{0:T(128)}, u32[]{:S(2)}) copy-start(f32[64]{0:T(128)} %param.23) | copy-start | bytes 772
  259.1 8.0 %copy-start.2 = (f32[1,4,1,32,4096]{4,3,1,2,0:T(8,128)S(1)}, f32[1,4,1,32,4096]{4,3,1,2,0:T(8,128)}, u32[]{:S(2)}) copy-start(f32[1,4,1,32,4096]{4,3,1,2,0:T(8,128)} %bitcast_convert_fusion) | copy-start | bytes 6291460
  259.1 8.0 %copy-start.9 = (f32[4096]{0:T(1024)S(1)}, f32[4096]{0:T(1024)}, u32[]{:S(2)}) copy-start(f32[4096]{0:T(1024)} %param.26) | copy-start | bytes 49156
  270.4 0.7 copy-start.19
  270.4 3.2 copy-start.13
  270.4 246.4 %all-gather.8.cloned.1.call-start = ((), (), s32[]{:S(2)}) async-start(), calls=%async_computation.5 | async-start | bytes 18874368 | tf_op jit(solution)/shard_map/all_gather | solution.py:184
  516.8 9.5 %copy-start.1 = (bf16[1,4,1,32,64]{4,3,2,1,0:T(8,128)(2,1)S(1)}, bf16[1,4,1,32,64]{4,3,2,1,0:T(8,128)(2,1)}, u32[]{:S(2)}) copy-start(bf16[1,4,1,32,64]{4,3,2,1,0:T(8,128)(2,1)} %param.20) | copy-start | bytes 49156
Sparse Core Ops, SparseCore 0:
  77.4 164.3 all-gather.9
  244.2 86.2 all-reduce.2
  332.1 32.1 all-gather.5
  365.7 151.0 all-gather.7
where the time goes:
time: 534 us; the launch traced here: 533 us
  waiting for transfers between devices  374 us (70%)
  local copies, waits for them, and re-layouts  36.1 us (7%)
  blocking collectives  34.7 us (6%)
  starting transfers between devices  25.4 us (5%)
  other arithmetic  24.6 us (5%)
  matrix products  21.1 us (4%)
  between operations  16.6 us (3%)
    all_gather x1, waiting for transfers between devices, local(): lax.all_gather(out_weight, ('seq', 'rep'), axis=0, tiled=True)  153 us
    all_gather x1, waiting for transfers between devices, prefix(): everything = jax.tree.map(lambda part: lax.all_gather(part, axis), value)  87.4 us
    all_to_all x1, waiting for transfers between devices, local(): lax.all_to_all(gate_proj, 'seq', split_axis=1, concat_axis=2, tiled=True)  48.3 us
    psum x1, waiting for transfers between devices, local(): final_state = lax.psum(after_decay[:, None, None] * local_final, 'seq')  37.3 us
    all_gather x1, waiting for transfers between devices, local(): features = lax.all_gather(normed, 'head', axis=1, tiled=True)  30.6 us
    psum x1, blocking collectives, broadcast(): return lax.psum(block, axis)  18.3 us
    all_to_all x1, waiting for transfers between devices, local(): lax.all_to_all(x_proj, 'seq', split_axis=1, concat_axis=2, tiled=True)  16.6 us
    all_gather x1, blocking collectives, prefix(): everything = jax.tree.map(lambda part: lax.all_gather(part, axis), value)  11.5 us
  transfers between devices with their start and end apart: 10, of which 8 were waited for; matrix products, arithmetic and copies ran while one was open for 12% of the time, Pallas kernels for 0%

commit v1 on v0

--- a/solution.py
+++ b/solution.py
@@ -171,7 +171,9 @@
     ).astype(jnp.bfloat16)
     last_index = seq_count - 1
     after_decay = prefix(dev_decay, "seq", multiply, ones_heads, True)
-    final_state = lax.psum(after_decay[:, None, None] * local_final, "seq")
+    own = after_decay[:, None, None] * local_final
+    parts = lax.all_gather(own, "seq")
+    final_state = jnp.sum(parts, axis=0)
     keep_x, keep_bc = (broadcast(tail_x, "seq", last_index), broadcast(tail_bc, "seq", last_index))
     slab_index = jnp.sum(
         jnp.where(owner[0] == seq_index, jnp.arange(seq_count, dtype=jnp.int32), 0)

time: 534 us -> 597 us (1.12)
  waiting for transfers between devices: 374 us -> 423 us
  blocking collectives: 34.7 us -> 45.5 us
    all_gather x0 -> x1, waiting for transfers between devices: none -> 88.9 us  [local(): parts = lax.all_gather(own, 'seq')]
    psum x1 -> x0, waiting for transfers between devices: 37.3 us -> none  [local(): final_state = lax.psum(after_decay[:, None, None] * local_final, 'seq')]
    psum x1, blocking collectives: 18.3 us -> 29.1 us  [broadcast(): return lax.psum(block, axis)]
    all_gather x1, waiting for transfers between devices: 30.6 us -> 23.3 us  [local(): features = lax.all_gather(normed, 'head', axis=1, tiled=True)]
  transfers between devices with their start and end apart: 10 -> 10, of which waited for: 8 -> 8; matrix products, arithmetic and copies ran while one was open for 12% -> 11% of each run, Pallas kernels for 0% -> 0%
where the time goes in v1:
time: 597 us; the launch traced here: 596 us
  waiting for transfers between devices  423 us (71%)
  blocking collectives  45.5 us (8%)
  local copies, waits for them, and re-layouts  33.9 us (6%)
  other arithmetic  29.4 us (5%)
  starting transfers between devices  25.4 us (4%)
  matrix products  22.3 us (4%)
  between operations  16.6 us (3%)
    all_gather x1, waiting for transfers between devices, local(): lax.all_gather(out_weight, ('seq', 'rep'), axis=0, tiled=True)  153 us
    all_gather x1, waiting for transfers between devices, prefix(): everything = jax.tree.map(lambda part: lax.all_gather(part, axis), value)  91 us
    all_gather x1, waiting for transfers between devices, local(): parts = lax.all_gather(own, 'seq')  88.9 us
    all_to_all x1, waiting for transfers between devices, local(): lax.all_to_all(gate_proj, 'seq', split_axis=1, concat_axis=2, tiled=True)  48.3 us
    psum x1, blocking collectives, broadcast(): return lax.psum(block, axis)  29.1 us
    all_gather x1, waiting for transfers between devices, local(): features = lax.all_gather(normed, 'head', axis=1, tiled=True)  23.3 us
    all_to_all x1, waiting for transfers between devices, local(): lax.all_to_all(x_proj, 'seq', split_axis=1, concat_axis=2, tiled=True)  16.7 us
  transfers between devices with their start and end apart: 10, of which 8 were waited for; matrix products, arithmetic and copies ran while one was open for 11% of the time, Pallas kernels for 0%

profile of v1, /device:TPU:0, one launch (start us, length us, event | category | flops | bytes accessed | tf_op | source)
XLA Modules:
  0.0 595.8 jit_solution(2211833884249454582)
XLA Ops:
  7.2 0.7 copy-done
  7.9 0.7 reshape.457
  8.6 6.3 %all-to-all-start.2 = ((bf16[4,2,1024]{2,1,0:T(2,128)(2,1)}), bf16[4,2,1024]{2,1,0:T(2,128)(2,1)S(1)}, u32[]{:S(2)}, u32[]{:S(2)}) async-start(bf16[4,2,1024]{2,1,0:T(2,128)(2,1)} %reshape.457), calls=%async_computation.2 | async-start | bytes 32768 | tf_op jit(solution)/shard_map/all_to_all | solution.py:111
  15.6 1.7 fusion.36
  17.3 1.4 fusion.37
  20.6 4.5 all-to-all-start.1
  25.2 0.7 broadcast_multiply_fusion.1
  26.1 0.7 bitcast_exponential_fusion
  27.1 1.8 copy.80
  28.9 11.5 %all-gather = f32[4,1,64]{2,1,0:T(1,128)S(1)} all-gather(f32[1,1,64]{2,1,0:T(1,128)S(1)} %get-tuple-element.290), channel_id=2, replica_groups=mesh['grp'=2,'seq'=4,'head'=2,'rep'=2] {'seq'}, dimensions={0}, use_global_device_ids=true | all-gather | bytes 1280 | tf_op jit(solution)/shard_map/all_gather | solution.py:23
  40.4 3.7 all-to-all-start
  44.9 0.9 bitcast_select_fusion.1
  46.4 3.8 collective-permute-start.1
  50.2 16.7 %all-to-all-done = bf16[1,4,1,32,4096]{4,3,2,0,1:T(8,128)(2,1)S(1)} async-done(((bf16[1,4,1,32,4096]{4,3,2,0,1:T(8,128)(2,1)}), bf16[1,4,1,32,4096]{4,3,2,0,1:T(8,128)(2,1)S(1)}, u32[]{:S(2)}, u32[]{:S(2)}) %all-to-all-start) | async-done | bytes 1048608 | tf_op jit(solution)/shard_map/all_to_all | solution.py:108
  67.2 1.3 collective-permute-start
  69.1 0.9 multiply_convert_fusion.4
  70.1 3.1 multiply_convert_fusion.2
  73.1 1.6 copy.81
  74.8 2.4 broadcast_multiply_fusion
  78.0 5.7 all-to-all-start.3
  84.2 48.3 %all-to-all-done.3 = bf16[1,4,1,32,4096]{4,3,2,0,1:T(8,128)(2,1)} async-done(((bf16[1,4,1,32,4096]{4,3,2,0,1:T(8,128)(2,1)}), bf16[1,4,1,32,4096]{4,3,2,0,1:T(8,128)(2,1)}, u32[]{:S(2)}, u32[]{:S(2)}) %all-to-all-start.3) | async-done | bytes 1048608 | tf_op jit(solution)/shard_map/all_to_all | solution.py:109
  132.5 2.7 bitcast_convert_fusion
  135.2 4.7 reshape.451
  139.9 4.8 copy.87
  144.7 1.3 copy.72
  146.0 1.7 copy.82
  147.7 3.9 fusion.1
  151.6 91.0 %all-gather.12.cloned.1.call-done = f32[256,64,128]{2,1,0:T(8,128)} async-done(((f32[64,64,128]{2,1,0:T(8,128)}), f32[256,64,128]{2,1,0:T(8,128)}) %all-gather.12.cloned.1.call-update) | async-done | bytes 8388624 | tf_op jit(solution)/shard_map/all_gather | solution.py:23
  242.6 11.7 %while.35 = (s32[]{:T(128)}, f32[64,64,128]{2,1,0:T(8,128)S(1)}, s32[]{:T(128)}, f32[4,64]{1,0:T(4,128)}, f32[4,64,64,128]{3,2,1,0:T(8,128)}, /*index=5*/s32[]{:T(128)}, s32[]{:T(128)}) while((s32[]{:T(128)}, f32[64,64,128]{2,1,0:T(8,128)S(1)}, s32[]{:T(128)}, f32[4,64]{1,0:T(4,128)}, f32[4,64,64,128]{3,2,1,0:T(8,128)}, ...), condition=%wide.region_2.3_spmd.clone, body=%wide.region_1.2_spmd.clone.sunk | while | flops 2097156 | bytes 6292329 | solution.py:36
  242.6 0.7 dynamic-slice_bitcast_fusion.4
  243.3 2.1 fusion.44
  246.0 2.1 fusion.44
  248.8 2.3 fusion.44
  251.2 0.7 dynamic-slice_bitcast_fusion.4
  251.9 2.3 fusion.44
  254.3 6.4 %multiply_reduce_fusion = (f32[128]{0:T(128)S(1)}, f32[1,128,64,64]{1,3,2,0:T(8,128)}) fusion(f32[1,128,64,64]{1,3,2,0:T(8,128)} %copy.87, f32[1,128,64,64]{1,3,2,0:T(8,128)} %bitcast.135, f32[64]{0:T(128)S(1)} %copy-done.17, f32[64,64,128]{2,1,0:T(8,128)S(1)} %get-tuple-element.223, bf16[128,256]{1,0:T(8,128)(2,1)S(1)} %multiply_convert_fusion.4, ...), kind=kOutput, calls=%fused_computation.17 | convolution fusion | flops 811073408 | bytes 10552320 | tf_op jit(solution)/shard_map/kqn,khpn->kqhp/dot_general | solution.py:162
  260.7 3.1 copy.85
  263.7 4.9 psum.21
  268.6 3.3 fusion.14
  275.2 29.1 %all-reduce = (bf16[3,4,1024]{2,0,1:T(4,128)(2,1)S(1)}, bf16[3,4,64]{2,0,1:T(4,128)(2,1)S(1)}) all-reduce(bf16[3,4,1024]{2,0,1:T(4,128)(2,1)S(1)} %bitcast.142, bf16[3,4,64]{2,0,1:T(4,128)(2,1)S(1)} %copy.89), channel_id=1, replica_groups=mesh['grp'=2,'seq'=4,'head'=2,'rep'=2] {'seq'}, use_global_device_ids=true, to_apply=%region_9.10 | all-reduce | flops 13056 | bytes 52224 | tf_op jit(solution)/shard_map/psum | solution.py:41
  305.5 88.9 %all-gather.14.cloned.1.call-done = f32[256,64,128]{2,1,0:T(8,128)} async-done(((f32[64,64,128]{2,1,0:T(8,128)}), f32[256,64,128]{2,1,0:T(8,128)}) %all-gather.14.cloned.1.call-update) | async-done | bytes 8388624 | tf_op jit(solution)/shard_map/all_gather | solution.py:175
  394.3 4.6 reduce_sum.28
  398.9 1.7 reshape_reshape.3
  400.6 2.4 constant_dynamic-slice_fusion
  403.0 1.0 copy.92
  404.0 23.3 %all-gather.8.cloned.1.call-done = bf16[128,8192]{1,0:T(8,128)(2,1)} async-done(((bf16[128,4096]{1,0:T(8,128)(2,1)}), bf16[128,8192]{1,0:T(8,128)(2,1)}) %all-gather.8.cloned.1.call-update) | async-done | bytes 2097168 | tf_op jit(solution)/shard_map/all_gather | solution.py:184
  427.2 152.6 %all-gather.10.cloned.1.call-done = bf16[8192,1024]{1,0:T(8,128)(2,1)} async-done(((bf16[1024,1024]{1,0:T(8,128)(2,1)}), bf16[8192,1024]{1,0:T(8,128)(2,1)}) %all-gather.10.cloned.1.call-update) | async-done | bytes 16777232 | tf_op jit(solution)/shard_map/all_gather | solution.py:186
  579.8 9.5 %fusion.16 = bf16[1,128,1024]{2,1,0:T(8,128)(2,1)} fusion(bf16[128,8192]{1,0:T(8,128)(2,1)} %all-gather.8.cloned.1.call-done, bf16[8192,1024]{1,0:T(8,128)(2,1)} %all-gather.10.cloned.1.call-done), kind=kOutput, calls=%fused_computation.31 | convolution fusion | flops 2147614720 | bytes 19136512 | tf_op jit(solution)/shard_map/dot_general | solution.py:84
  (82 shorter events, 9.8 us)
Async XLA Ops:
  7.2 0.8 copy-start
  8.6 12.0 %all-to-all-start.2 = ((bf16[4,2,1024]{2,1,0:T(2,128)(2,1)}), bf16[4,2,1024]{2,1,0:T(2,128)(2,1)S(1)}, u32[]{:S(2)}, u32[]{:S(2)}) async-start(bf16[4,2,1024]{2,1,0:T(2,128)(2,1)} %reshape.457), calls=%async_computation.2 | async-start | bytes 32768 | tf_op jit(solution)/shard_map/all_to_all | solution.py:111
  19.3 7.5 %copy-start.10 = (f32[128]{0:T(128)}, f32[128]{0:T(128)S(1)}, u32[]{:S(2)}) copy-start(f32[128]{0:T(128)S(1)} %get-tuple-element.282) | copy-start | bytes 1540
  20.6 19.8 %all-to-all-start.1 = ((bf16[1,4,1,32,256]{4,3,2,0,1:T(8,128)(2,1)}), bf16[1,4,1,32,256]{4,3,2,0,1:T(8,128)(2,1)S(1)}, u32[]{:S(2)}, u32[]{:S(2)}) async-start(bf16[1,4,1,32,256]{4,3,2,0,1:T(8,128)(2,1)} %bitcast.147), calls=%async_computation.1 | async-start | bytes 131072 | tf_op jit(solution)/shard_map/all_to_all | solution.py:110
  28.9 15.8 %copy-start.5 = (f32[64]{0:T(128)S(1)}, f32[64]{0:T(128)}, u32[]{:S(2)}) copy-start(f32[64]{0:T(128)} %custom-call.1) | copy-start | bytes 772
  28.9 15.9 %copy-start.14 = (pred[128]{0:T(512)(128)(4,1)S(1)}, pred[128]{0:T(512)(128)(4,1)}, u32[]{:S(2)}) copy-start(pred[128]{0:T(512)(128)(4,1)} %get-tuple-element.283) | copy-start | bytes 388
  40.4 4.4 copy-start.4
  40.4 29.6 %copy-start.3 = (f32[128,4096]{1,0:T(8,128)S(1)}, f32[128,4096]{1,0:T(8,128)}, u32[]{:S(2)}) copy-start(f32[128,4096]{1,0:T(8,128)} %copy.80) | copy-start | bytes 6291460
  40.4 26.5 %all-to-all-start = ((bf16[1,4,1,32,4096]{4,3,2,0,1:T(8,128)(2,1)}), bf16[1,4,1,32,4096]{4,3,2,0,1:T(8,128)(2,1)S(1)}, u32[]{:S(2)}, u32[]{:S(2)}) async-start(bf16[1,4,1,32,4096]{4,3,2,0,1:T(8,128)(2,1)} %bitcast.137), calls=%async_computation | async-start | bytes 2097152 | tf_op jit(solution)/shard_map/all_to_all | solution.py:108
  44.1 198.5 %all-gather.12.cloned.1.call-start = ((), (), s32[]{:S(2)}) async-start(), calls=%async_computation.6 | async-start | bytes 10485760 | tf_op jit(solution)/shard_map/all_gather | solution.py:23
  44.8 22.1 %copy-start.6 = (f32[64]{0:T(128)}, f32[64]{0:T(128)S(1)}, u32[]{:S(2)}) copy-start(f32[64]{0:T(128)S(1)} %get-tuple-element.224) | copy-start | bytes 772
  44.8 22.1 %copy-start.9 = (f32[4,64]{1,0:T(4,128)}, f32[4,64]{1,0:T(4,128)S(1)}, u32[]{:S(2)}) copy-start(f32[4,64]{1,0:T(4,128)S(1)} %get-tuple-element.430) | copy-start | bytes 3076
  46.4 22.1 %collective-permute-start.1 = (bf16[3,256]{1,0:T(4,128)(2,1)S(1)}, bf16[3,256]{1,0:T(4,128)(2,1)S(1)}, u32[]{:S(2)}, u32[]{:S(2)}) collective-permute-start(bf16[3,256]{1,0:T(4,128)(2,1)S(1)} %get-tuple-element.287), channel_id=1, source_target_pairs={{0,4},{4,8},{8,12},{1,5},{5,9},{9,13},{2,6},{6,10},{10,14},{3,7},{... | collective-permute-start | bytes 4616 | tf_op jit(solution)/shard_map/ppermute | solution.py:18
  67.2 2.9 collective-permute-start
  68.5 0.6 copy-start.15
  73.1 1.6 copy-start.7
  73.1 1.6 copy-start.16
  77.2 317.1 %all-gather.14.cloned.1.call-start = ((), (), s32[]{:S(2)}) async-start(), calls=%async_computation.7 | async-start | bytes 10485760 | tf_op jit(solution)/shard_map/all_gather | solution.py:175
  77.3 6.4 %copy-start.11 = (f32[128]{0:T(128)S(1)}, f32[128]{0:T(128)}, u32[]{:S(2)}) copy-start(f32[128]{0:T(128)} %copy-done.10) | copy-start | bytes 1540
  77.3 6.4 %copy-start.13 = (f32[64]{0:T(128)S(1)}, f32[64]{0:T(128)}, u32[]{:S(2)}) copy-start(f32[64]{0:T(128)} %param.22) | copy-start | bytes 772
  78.0 54.5 %all-to-all-start.3 = ((bf16[1,4,1,32,4096]{4,3,2,0,1:T(8,128)(2,1)}), bf16[1,4,1,32,4096]{4,3,2,0,1:T(8,128)(2,1)}, u32[]{:S(2)}, u32[]{:S(2)}) async-start(bf16[1,4,1,32,4096]{4,3,2,0,1:T(8,128)(2,1)} %bitcast.35), calls=%async_computation.3 | async-start | bytes 2097152 | tf_op jit(solution)/shard_map/all_to_all | solution.py:109
  83.7 343.6 %all-gather.8.cloned.1.call-start = ((), (), s32[]{:S(2)}) async-start(), calls=%async_computation.4 | async-start | bytes 3145728 | tf_op jit(solution)/shard_map/all_gather | solution.py:184
  242.6 11.7 %copy-start.17 = (f32[64]{0:T(128)S(1)}, f32[64]{0:T(128)}, u32[]{:S(2)}) copy-start(f32[64]{0:T(128)} %param.23) | copy-start | bytes 772
  260.6 8.0 %copy-start.2 = (f32[1,4,1,32,4096]{4,3,1,2,0:T(8,128)S(1)}, f32[1,4,1,32,4096]{4,3,1,2,0:T(8,128)}, u32[]{:S(2)}) copy-start(f32[1,4,1,32,4096]{4,3,1,2,0:T(8,128)} %bitcast_convert_fusion) | copy-start | bytes 6291460
  260.7 8.0 %copy-start.8 = (f32[4096]{0:T(1024)S(1)}, f32[4096]{0:T(1024)}, u32[]{:S(2)}) copy-start(f32[4096]{0:T(1024)} %param.26) | copy-start | bytes 49156
  271.9 0.7 copy-start.18
  271.9 3.2 copy-start.12
  271.9 307.9 %all-gather.10.cloned.1.call-start = ((), (), s32[]{:S(2)}) async-start(), calls=%async_computation.5 | async-start | bytes 18874368 | tf_op jit(solution)/shard_map/all_gather | solution.py:186
  579.8 9.5 %copy-start.1 = (bf16[1,4,1,32,64]{4,3,2,1,0:T(8,128)(2,1)S(1)}, bf16[1,4,1,32,64]{4,3,2,1,0:T(8,128)(2,1)}, u32[]{:S(2)}) copy-start(bf16[1,4,1,32,64]{4,3,2,1,0:T(8,128)(2,1)} %param.20) | copy-start | bytes 49156
Sparse Core Ops, SparseCore 0:
  77.4 165.1 all-gather.11
  244.1 150.1 all-gather.13
  395.9 31.3 all-gather.7
  428.7 151.0 all-gather.9
